TPU v7x, 512 devices: a 4x2x32 block of a 4x8x32 slice. The times are simulated.
512 devices in a mesh: grp: 2 (over y), row: 32 (over z), col: 4 (over x), ch: 2 (over core).
Axes of the slice: x: 4, y: 2, z: 32, core: 2. Of those that a mesh axis runs over, the one named last changes fastest.
The devices are a block of a 4x8x32 slice.
Arguments:
- pair_act: bfloat16 [128, 1024, 512], P('ch', ('grp', 'row'), 'col'), parts along dimension 1, may hold values from -48 to 48
- in_gain: float32 [128], P('ch'), may hold values from 0.1 to 1.9
- left_proj: bfloat16 [128, 128], P(None, 'ch'), may hold values from -0.5 to 0.5
- left_gate: bfloat16 [128, 128], P(None, 'ch'), may hold values from -0.5 to 0.5
- right_proj: bfloat16 [128, 128], P(None, 'ch'), may hold values from -0.5 to 0.5
- right_gate: bfloat16 [128, 128], P(None, 'ch'), may hold values from -0.5 to 0.5
- out_gate: bfloat16 [128, 128], P(None, 'ch'), may hold values from -0.5 to 0.5
- out_gain: float32 [128], P('ch'), may hold values from 0.1 to 1.9
- out_proj: bfloat16 [128, 128], P(None, 'ch'), may hold values from -0.5 to 0.5
Outputs:
- update: bfloat16 [128, 1024, 512], P('ch', ('grp', 'row'), 'col'), parts along dimension 1
There are 2 independent parts, one for each index of `grp`. A program takes and returns all parts, laid end to end along the dimension named above; an argument that names none is the same for every part. Nothing has to cross between parts.
All inputs are finite; a program needn't handle non-finite values.
Results may differ from a plain program's by a relative error of at most 0.0085.
Values may be sent and summed in bfloat16 or wider, within the bound.
A program may use at most 64 MiB of HBM per device.

v0:
```python
import jax
import jax.numpy as jnp
from jax import lax
from jax.sharding import PartitionSpec as P


def copy_for_each(x, axis):
    copies = jnp.broadcast_to(x, (lax.axis_size(axis), *x.shape))
    return lax.all_to_all(copies, axis, split_axis=0, concat_axis=0, tiled=True)


def taken_together(x, axis):
    return copy_for_each(x, axis).sum(axis=0)


def in_one(arrays, axis):
    ends = [0]
    for a in arrays:
        ends.append(ends[-1] + a.size)
    total = taken_together(jnp.concatenate([a.ravel() for a in arrays]), axis)
    return tuple((total[b:e].reshape(a.shape) for a, b, e in zip(arrays, ends, ends[1:])))


def joined_along(pieces, dim):
    shape = list(pieces.shape[1:])
    shape[dim] *= pieces.shape[0]
    return jnp.moveaxis(pieces, 0, dim).reshape(shape)


def gather_directly(x, axis, dim):
    return joined_along(copy_for_each(x, axis), dim)


def moments(values, channel_count):
    first_sums, squares = in_one((jnp.sum(values, axis=0), jnp.sum(values * values, axis=0)), "ch")
    average = first_sums / channel_count
    spread = squares / channel_count - average * average
    centred = values - average[None]
    return centred * lax.rsqrt(spread + 1e-05)[None]


def per_device(
    pair_act, in_gain, left_proj, left_gate, right_proj, right_gate, out_gate, out_gain, out_proj
):
    row_count = pair_act.shape[1]
    hidden = left_proj.shape[1]
    normed = (
        moments(pair_act.astype(jnp.float32), pair_act.shape[0] * lax.axis_size("ch"))
        * in_gain[:, None, None]
    ).astype(jnp.bfloat16)
    whole = gather_directly(normed, "ch", 0)
    left_weights = jnp.concatenate((left_proj, left_gate), axis=1)
    left_lifted = jnp.einsum("cxy,cn->nyx", whole, left_weights, preferred_element_type=jnp.float32)
    left_edge = (jax.nn.sigmoid(left_lifted[hidden:]) * left_lifted[:hidden]).astype(jnp.bfloat16)
    other_weights = jnp.concatenate((right_proj, right_gate, out_gate), axis=1)
    other_lifted = jnp.einsum(
        "cxy,cn->nxy", whole, other_weights, preferred_element_type=jnp.float32
    )
    right_edge = (jax.nn.sigmoid(other_lifted[hidden : 2 * hidden]) * other_lifted[:hidden]).astype(
        jnp.bfloat16
    )
    gate_map = jax.nn.sigmoid(other_lifted[2 * hidden :])
    across = gather_directly(left_edge, "col", 1)
    blocks = across.reshape(hidden, lax.axis_size("row"), row_count, row_count)
    arrived = lax.all_to_all(blocks, "row", split_axis=1, concat_axis=3, tiled=True)
    left_panel = arrived.reshape(hidden, row_count, -1)
    tri_sum = jnp.einsum(
        "hik,hkj->hij",
        left_panel,
        lax.all_gather(right_edge, "row", axis=1, tiled=True),
        preferred_element_type=jnp.float32,
    )
    mid_norm = (moments(tri_sum, hidden * lax.axis_size("ch")) * out_gain[:, None, None]).astype(
        jnp.bfloat16
    )
    all_mid = gather_directly(mid_norm, "ch", 0)
    projected = jnp.einsum("hxy,hc->cxy", all_mid, out_proj, preferred_element_type=jnp.float32)
    return (gate_map * projected).astype(jnp.bfloat16)


def solution(mesh):
    return jax.shard_map(
        per_device,
        mesh=mesh,
        in_specs=(
            P("ch", ("grp", "row"), "col"),
            P("ch"),
            P(None, "ch"),
            P(None, "ch"),
            P(None, "ch"),
            P(None, "ch"),
            P(None, "ch"),
            P("ch"),
            P(None, "ch"),
        ),
        out_specs=P("ch", ("grp", "row"), "col"),
        check_vma=False,
    )
```

profile of v0, /device:TPU:33, one launch (start us, length us, event | category | flops | bytes accessed | tf_op | source)
XLA Modules:
  0.0 320.6 jit_solution(7543671006163515305)
XLA Ops:
  6.6 1.1 convert_reduce_fusion
  7.6 0.0 copy-start.3
  7.7 44.8 %all_to_all.42 = f32[2,1,4096]{2,1,0:T(1,128)S(1)} all-to-all(f32[2,1,4096]{2,1,0:T(1,128)S(1)} %broadcast_in_dim.10), channel_id=1, replica_groups=mesh['grp'=2,'row'=32,'col'=4,'ch'=2] {'ch'}, dimensions={0} | all-to-all | bytes 65536 | tf_op jit(solution)/shard_map/all_to_all | solution.py:9
  52.6 1.1 fusion.7
  53.7 0.1 copy.43
  53.8 0.1 broadcast_in_dim.22
  53.9 4.1 %all_to_all.43 = bf16[2,64,16,128]{3,1,2,0:T(8,128)(2,1)S(1)} all-to-all(bf16[2,64,16,128]{3,1,2,0:T(8,128)(2,1)S(1)} %broadcast_in_dim.22), channel_id=1, replica_groups=mesh['grp'=2,'row'=32,'col'=4,'ch'=2] {'ch'}, dimensions={0} | all-to-all | bytes 1048576 | tf_op jit(solution)/shard_map/all_to_all | solution.py:9
  58.2 0.4 fusion.19
  58.5 1.2 copy-done.1
  59.7 0.8 fusion.8
  60.6 0.1 all-gather.2.cloned.1.call-update
  60.7 0.3 convolution_bitcast_fusion
  61.0 0.1 fusion.12
  61.1 0.2 copy.45
  61.3 0.1 broadcast_in_dim.23
  61.4 17.3 %all_to_all.44 = bf16[4,64,128,16]{2,3,1,0:T(8,128)(2,1)S(1)} all-to-all(bf16[4,64,128,16]{2,3,1,0:T(8,128)(2,1)S(1)} %broadcast_in_dim.23), channel_id=1, replica_groups=mesh['grp'=2,'row'=32,'col'=4,'ch'=2] {'col'}, dimensions={0} | all-to-all | bytes 2097152 | tf_op jit(solution)/shard_map/all_to_all | solution.py:9
  78.7 2.3 copy.46
  81.0 1.5 reshape.90
  82.5 123.0 %all_to_all.45 = bf16[32,2,8192]{2,1,0:T(2,128)(2,1)} all-to-all(bf16[32,2,8192]{2,1,0:T(2,128)(2,1)S(1)} %reshape.90), channel_id=1, replica_groups=mesh['grp'=2,'row'=32,'col'=4,'ch'=2] {'row'}, dimensions={0} | all-to-all | bytes 2097152 | tf_op jit(solution)/shard_map/all_to_all | solution.py:65
  205.4 3.8 %reshape.91 = bf16[32,16,16,64]{3,2,1,0:T(8,128)(2,1)S(1)} reshape(bf16[32,2,8192]{2,1,0:T(2,128)(2,1)} %all_to_all.45) | data formatting | bytes 2097152
  209.2 0.4 bitcast_bitcast_fusion
  209.6 0.5 copy.47
  210.1 1.8 copy.48
  211.9 54.8 %all-gather.2.cloned.1.call-done = bf16[64,512,128]{2,0,1:T(8,128)(2,1)} async-done(((bf16[64,16,128]{2,0,1:T(8,128)(2,1)}), bf16[64,512,128]{2,0,1:T(8,128)(2,1)}) %all-gather.2.cloned.1.call-update) | async-done | bytes 8388624 | tf_op jit(solution)/shard_map/all_gather | solution.py:70
  266.7 20.1 %fusion.39 = (f32[16,128]{1,0:T(8,128)S(1)}, f32[16,128]{1,0:T(8,128)S(1)}, f32[64,16,128]{2,1,0:T(8,128)S(1)}) fusion(bf16[64,16,512]{2,1,0:T(8,128)(2,1)S(1)} %copy.48, bf16[64,512,128]{2,0,1:T(8,128)(2,1)} %all-gather.2.cloned.1.call-done), kind=kOutput, calls=%fused_computation.59 | convolution fusion | flops 134606848 | bytes 9977856 | tf_op jit(solution)/shard_map/hik,hkj->hij/dot_general | solution.py:67
  286.8 20.1 %all_to_all.46 = f32[2,1,4096]{2,1,0:T(1,128)S(1)} all-to-all(f32[2,1,4096]{2,1,0:T(1,128)S(1)} %broadcast_in_dim.24), channel_id=1, replica_groups=mesh['grp'=2,'row'=32,'col'=4,'ch'=2] {'ch'}, dimensions={0} | all-to-all | bytes 65536 | tf_op jit(solution)/shard_map/all_to_all | solution.py:9
  307.0 0.1 multiply_convert_fusion
  307.1 0.1 copy.51
  307.2 0.1 broadcast_in_dim.25
  307.3 4.1 %all_to_all.47 = bf16[2,64,16,128]{3,1,2,0:T(8,128)(2,1)S(1)} all-to-all(bf16[2,64,16,128]{3,1,2,0:T(8,128)(2,1)S(1)} %broadcast_in_dim.25), channel_id=1, replica_groups=mesh['grp'=2,'row'=32,'col'=4,'ch'=2] {'ch'}, dimensions={0} | all-to-all | bytes 1048576 | tf_op jit(solution)/shard_map/all_to_all | solution.py:9
  311.5 1.3 fusion.3
  312.8 0.9 copy.53
  (27 shorter events, 0.3 us)
Async XLA Ops:
  6.5 305.0 %copy-start = (bf16[128,64]{0,1:T(8,128)(2,1)S(1)}, bf16[128,64]{0,1:T(8,128)(2,1)}, u32[]{:S(2)}) copy-start(bf16[128,64]{0,1:T(8,128)(2,1)} %param.17) | copy-start | bytes 49156
  6.6 260.1 %all-gather.2.cloned.1.call-start = ((), (), s32[]{:S(2)}) async-start(), calls=%async_computation.6 | async-start | bytes 8650752 | tf_op jit(solution)/shard_map/all_gather | solution.py:70
  7.6 50.5 %copy-start.2 = (bf16[128,64]{0,1:T(8,128)(2,1)S(1)}, bf16[128,64]{0,1:T(8,128)(2,1)}, u32[]{:S(2)}) copy-start(bf16[128,64]{0,1:T(8,128)(2,1)} %param.15) | copy-start | bytes 49156
  7.6 50.5 %copy-start.3 = (bf16[128,64]{0,1:T(8,128)(2,1)S(1)}, bf16[128,64]{0,1:T(8,128)(2,1)}, u32[]{:S(2)}) copy-start(bf16[128,64]{0,1:T(8,128)(2,1)} %param.14) | copy-start | bytes 49156
  7.6 50.5 %copy-start.4 = (bf16[128,64]{0,1:T(8,128)(2,1)S(1)}, bf16[128,64]{0,1:T(8,128)(2,1)}, u32[]{:S(2)}) copy-start(bf16[128,64]{0,1:T(8,128)(2,1)} %param.13) | copy-start | bytes 49156
  58.1 2.6 copy-start.5
  58.1 2.6 copy-start.6
  58.5 1.2 copy-start.1
  211.9 95.1 %copy-start.7 = (f32[64]{0:T(128)S(1)}, f32[64]{0:T(128)}, u32[]{:S(2)}) copy-start(f32[64]{0:T(128)} %param.16) | copy-start | bytes 772
Sparse Core Ops, SparseCore 0:
  60.8 205.8 all-gather.1
where the time goes:
time: 321 us
  blocking collectives  213 us (66%)
  waiting for transfers between devices  54.8 us (17%)
  matrix products  22 us (7%)
  between operations  13.7 us (4%)
  local copies, waits for them, and re-layouts  13.1 us (4%)
  other arithmetic  3.4 us (1%)
    all_to_all x1, blocking collectives, per_device(): lax.all_to_all(blocks, 'row', split_axis=1, concat_axis=3, tiled=True)  123 us
    all_to_all x5, blocking collectives, copy_for_each(): return lax.all_to_all(copies, axis, split_axis=0, concat_axis=0, tiled=True)  90.5 us
    all_gather x1, waiting for transfers between devices, per_device(): lax.all_gather(right_edge, 'row', axis=1, tiled=True)  54.8 us
    dot_general x1, matrix products, per_device(): jnp.einsum('hik,hkj->hij', left_panel, lax.all_gather(right_edge, 'row',...  20.1 us
    unnamed x18, local copies, waits for them, and re-layouts  6.49 us
  transfers between devices with their start and end apart: 1, of which 1 were waited for; matrix products, arithmetic and copies ran while one was open for 3% of the time, Pallas kernels for 0%

commit v1 on v0

v1 whole, which is shorter than its diff:
```python
import functools

import jax
import jax.numpy as jnp
from jax import lax
from jax.experimental import pallas as pl
from jax.experimental.pallas import tpu as pltpu
from jax.sharding import PartitionSpec as P

MESH = pl.DeviceIdType.MESH
EPS = 1e-05
F32, BF16 = jnp.float32, jnp.bfloat16


def kernel(n, nx, pa, ing, lp, lg, rp, rg, og, outg, op, out,
           other, gains, gains_other, gain_all, x_all, wt, gate, y_left, y_right,
           send, recv, left_all, tri_send, tri_recv, tri_other,
           ready, ready_x, ch_send, ch_recv, z_send, z_recv, x_send, x_recv, t_send, t_recv):
    z, x, c = lax.axis_index("row"), lax.axis_index("col"), lax.axis_index("ch")
    ch, rows, lanes = pa.shape
    hp = ch // n
    bar = pltpu.get_barrier_semaphore()

    def each(lo, hi, f):
        def step(i, carry):
            f(i)
            return carry
        lax.fori_loop(lo, hi, step, 0)

    pl.semaphore_signal(bar, inc=1, device_id={"ch": 1 - c}, device_id_type=MESH)
    each(z + 1, n, lambda r: pl.semaphore_signal(bar, inc=1, device_id={"row": r}, device_id_type=MESH))
    each(0, x, lambda r: pl.semaphore_signal(bar, inc=1, device_id={"col": r}, device_id_type=MESH))
    pl.semaphore_wait(bar, z + (nx - 1 - x) + 1)
    each(0, z, lambda r: pl.semaphore_signal(ready.at[z], inc=1, device_id={"row": r}, device_id_type=MESH))
    each(x + 1, nx, lambda r: pl.semaphore_signal(ready_x.at[x], inc=1, device_id={"col": r}, device_id_type=MESH))

    def to_core(src, dst, i):
        return pltpu.make_async_remote_copy(src_ref=src, dst_ref=dst, send_sem=ch_send.at[i], recv_sem=ch_recv.at[i],
                                            device_id={"ch": 1 - c}, device_id_type=MESH)

    raw = to_core(pa, other, 0)
    raw.start()
    for i, g in enumerate((ing, outg)):
        gains[i] = jnp.broadcast_to(g[...], (lanes, ch)).T
    for i, w in enumerate((lp, lg, rp, rg, og)):
        wt[pl.ds(i * ch, ch), :] = w[...]
    gsent = to_core(gains, gains_other, 1)
    gsent.start()
    mine = pl.multiple_of(c * ch, ch)
    theirs = pl.multiple_of((1 - c) * ch, ch)
    gsent.wait_recv()
    for i in range(2):
        gain_all[i, pl.ds(mine, ch), :] = gains[i]
        gain_all[i, pl.ds(theirs, ch), :] = gains_other[i]
    raw.wait_recv()

    step_c = 8

    def layer_norm(a, b):
        def add(i, t):
            s = pl.ds(i * step_c, step_c)
            return t + a[s].astype(F32).sum(0) + b[s].astype(F32).sum(0)
        mean = lax.fori_loop(0, ch // step_c, add, jnp.zeros((rows, lanes), F32)) / (2 * ch)

        def sq(i, t):
            s = pl.ds(i * step_c, step_c)
            return t + jnp.square(a[s].astype(F32) - mean).sum(0) + jnp.square(b[s].astype(F32) - mean).sum(0)
        var = lax.fori_loop(0, ch // step_c, sq, jnp.zeros((rows, lanes), F32)) / (2 * ch)
        scale = lax.rsqrt(var + EPS)

        def put(i, carry):
            s = pl.ds(i * step_c, step_c)
            for r, base in ((a, mine), (b, theirs)):
                v = (r[s].astype(F32) - mean) * scale
                x_all[pl.ds(pl.multiple_of((base + i * step_c) * rows, rows * step_c), rows * step_c), :] = v.reshape(rows * step_c, lanes)
            return carry
        lax.fori_loop(0, ch // step_c, put, 0)

    layer_norm(pa, other)

    def lift(k):
        v = (x_all[pl.ds(k, 2 * ch, stride=rows), :] * gain_all[0]).astype(BF16)
        r = jnp.dot(wt[...], v, preferred_element_type=F32)
        y_left[pl.ds(k, ch, stride=rows), :] = jax.nn.sigmoid(r[ch : 2 * ch]) * r[:ch]
        y_right[pl.ds(k, ch, stride=rows), :] = jax.nn.sigmoid(r[3 * ch : 4 * ch]) * r[2 * ch : 3 * ch]
        gate[k] = jax.nn.sigmoid(r[4 * ch :])
    each(0, rows, lift)

    def pack(i):
        s = pl.ds(pl.multiple_of(i * hp * rows, hp * rows), hp * rows)
        send[i, 0] = y_left[s, :].reshape(hp, rows, lanes).astype(BF16)
        send[i, 1] = y_right[s, :].reshape(hp, rows, lanes).astype(BF16)
    each(0, n, pack)

    def to_row(r):
        pltpu.make_async_remote_copy(src_ref=send.at[r], dst_ref=recv.at[z], send_sem=z_send, recv_sem=z_recv.at[z],
                                     device_id={"row": r}, device_id_type=MESH).start()

    def down_half(i):
        d = n // 2 - i
        r1, r2 = lax.rem(z + d, n), lax.rem(z + n - d, n)

        @pl.when(r1 < z)
        def _():
            to_row(r1)

        @pl.when((r2 < z) & (d < n // 2))
        def _():
            to_row(r2)
    each(0, n // 2, down_half)
    recv[z] = send[z]

    def up(r):
        pl.semaphore_wait(ready.at[r], 1)
        to_row(r)
    each(z + 1, n, up)

    each(0, x, lambda r: pl.semaphore_wait(ready_x.at[r], 1))

    def to_col(s, r):
        return pltpu.make_async_remote_copy(src_ref=recv.at[s, 0], dst_ref=left_all.at[x, s], send_sem=x_send, recv_sem=x_recv.at[x],
                                            device_id={"col": r}, device_id_type=MESH)

    def spread(s):
        @pl.when(s != z)
        def _():
            pltpu.make_async_remote_copy(src_ref=send.at[s], dst_ref=recv.at[s], send_sem=z_send, recv_sem=z_recv.at[s],
                                         device_id={"row": s}, device_id_type=MESH).wait_recv()
        for d in range(1, nx):
            to_col(s, lax.rem(x + d, nx)).start()
        left_all[x, s] = recv[s, 0]
    each(0, n, spread)

    for d in range(1, nx):
        r = lax.rem(x + d, nx)
        pltpu.make_async_remote_copy(src_ref=left_all.at[r], dst_ref=left_all.at[r], send_sem=x_send, recv_sem=x_recv.at[r],
                                     device_id={"col": r}, device_id_type=MESH).wait_recv()

    per = lanes // rows
    for h in range(hp):
        right = recv[:, 1, h].reshape(n * rows, lanes)
        for q in range(nx):
            left = left_all[q, :, h].reshape(n * rows, lanes)
            t = lax.dot_general(left, right, (((0,), (0,)), ((), ())), preferred_element_type=F32)
            tri_send[pl.ds(q * per, per), h] = t.reshape(per, rows, lanes).astype(BF16)

    def tri_to(r):
        pltpu.make_async_remote_copy(src_ref=tri_send.at[r], dst_ref=tri_recv.at[z], send_sem=t_send, recv_sem=t_recv,
                                     device_id={"row": r}, device_id_type=MESH).start()

    def tri_out(i):
        d = n // 2 - i
        tri_to(lax.rem(z + d, n))

        @pl.when(d < n // 2)
        def _():
            tri_to(lax.rem(z + n - d, n))
    each(0, n // 2, tri_out)
    tri_recv[z] = tri_send[z]
    most = pl.ds(0, n - 1)
    pltpu.make_async_remote_copy(src_ref=tri_send.at[most], dst_ref=tri_recv.at[most], send_sem=t_send, recv_sem=t_recv,
                                 device_id={"row": lax.rem(z + 1, n)}, device_id_type=MESH).wait_recv()

    swap = to_core(tri_recv, tri_other, 2)
    swap.start()
    swap.wait_recv()
    layer_norm(tri_recv.reshape(ch, rows, lanes), tri_other.reshape(ch, rows, lanes))

    def close(k):
        v = (x_all[pl.ds(k, 2 * ch, stride=rows), :] * gain_all[1]).astype(BF16)
        y_left[pl.ds(k, ch, stride=rows), :] = jnp.dot(op[...], v, preferred_element_type=F32) * gate[k]
    each(0, rows, close)
    out[...] = y_left[...].reshape(ch, rows, lanes).astype(BF16)

    raw.wait_send()
    gsent.wait_send()
    swap.wait_send()
    pltpu.make_async_remote_copy(src_ref=send.at[most], dst_ref=recv.at[most], send_sem=z_send, recv_sem=z_recv.at[z],
                                 device_id={"row": lax.rem(z + 1, n)}, device_id_type=MESH).wait_send()
    pltpu.make_async_remote_copy(src_ref=tri_send.at[most], dst_ref=tri_recv.at[most], send_sem=t_send, recv_sem=t_recv,
                                 device_id={"row": lax.rem(z + 1, n)}, device_id_type=MESH).wait_send()
    for d in range(1, nx):
        r = lax.rem(x + d, nx)
        pltpu.make_async_remote_copy(src_ref=left_all.at[r], dst_ref=left_all.at[r], send_sem=x_send, recv_sem=x_recv.at[r],
                                     device_id={"col": r}, device_id_type=MESH).wait_send()


def solution(mesh):
    n, nx = mesh.shape["row"], mesh.shape["col"]

    def per_device(pair_act, in_gain, left_proj, left_gate, right_proj, right_gate, out_gate, out_gain, out_proj):
        ch, rows, lanes = pair_act.shape
        hp = ch // n
        vm = pltpu.VMEM
        dma, reg = pltpu.SemaphoreType.DMA, pltpu.SemaphoreType.REGULAR
        return pl.pallas_call(
            functools.partial(kernel, n, nx),
            out_shape=jax.ShapeDtypeStruct(pair_act.shape, BF16),
            in_specs=[pl.BlockSpec(memory_space=pltpu.VMEM)] * 9,
            out_specs=pl.BlockSpec(memory_space=pltpu.VMEM),
            scratch_shapes=[
                vm((ch, rows, lanes), BF16),
                vm((2, ch, lanes), F32),
                vm((2, ch, lanes), F32),
                vm((2, 2 * ch, lanes), F32),
                vm((2 * ch * rows, lanes), F32),
                vm((5 * ch, 2 * ch), BF16),
                vm((rows, ch, lanes), F32),
                vm((ch * rows, lanes), F32),
                vm((ch * rows, lanes), F32),
                vm((n, 2, hp, rows, lanes), BF16),
                vm((n, 2, hp, rows, lanes), BF16),
                vm((nx, n, hp, rows, lanes), BF16),
                vm((n, hp, rows, lanes), BF16),
                vm((n, hp, rows, lanes), BF16),
                vm((n, hp, rows, lanes), BF16),
                reg((n,)),
                reg((nx,)),
                dma((3,)),
                dma((3,)),
                dma,
                dma((n,)),
                dma,
                dma((nx,)),
                dma,
                dma,
            ],
            compiler_params=pltpu.CompilerParams(collective_id=0, has_side_effects=True),
            name="triangle",
        )(pair_act, in_gain[None], left_proj.T, left_gate.T, right_proj.T, right_gate.T, out_gate.T, out_gain[None], out_proj.T)

    return jax.shard_map(
        per_device,
        mesh=mesh,
        in_specs=(
            P("ch", ("grp", "row"), "col"),
            P("ch"),
            P(None, "ch"),
            P(None, "ch"),
            P(None, "ch"),
            P(None, "ch"),
            P(None, "ch"),
            P("ch"),
            P(None, "ch"),
        ),
        out_specs=P("ch", ("grp", "row"), "col"),
        check_vma=False,
    )
```

time: 321 us -> 147 us (0.46)
  the two profiles are of different devices: /device:TPU:33 before, /device:TPU:35 now
where the time goes in v1:
time: 147 us
  Pallas kernels  145 us (99%)
  local copies, waits for them, and re-layouts  1.67 us (1%)
    pallas_call x1, Pallas kernels, per_device(): pl.pallas_call(functools.partial(kernel, n, nx), out_shape=jax.ShapeDtype...  145 us

profile of v1, /device:TPU:35, one launch (start us, length us, event | category | flops | bytes accessed | tf_op | source)
XLA Modules:
  0.0 146.8 jit_solution(11512508872851759453)
XLA Ops:
  0.0 145.1 %triangle.1 = bf16[64,16,128]{2,1,0:T(8,128)(2,1)} custom-call(bf16[64,16,128]{2,1,0:T(8,128)(2,1)} %pa.1, f32[1,64]{1,0:T(1,128)} %bitcast.14, bf16[64,128]{1,0:T(8,128)(2,1)} %bitcast.8, bf16[64,128]{1,0:T(8,128)(2,1)} %bitcast.9, bf16[64,128]{1,0:T(8,128)(2,1)} %bitcast.10, bf16[64,128]{1,0:T(8,128)(2,1)} %bitcast.11, bf16[64,128]{1,0:T(8,128)(2,1)} %bitcast.12, ...), custom_call_target="tpu_custom_call" | custom-call | tf_op jit(solution)/shard_map/triangle/pallas_call | solution.py:196
  145.1 1.7 %copy.11 = bf16[64,16,128]{2,1,0:T(8,128)(2,1)} copy(bf16[64,16,128]{2,1,0:T(8,128)(2,1)} %triangle.1) | data formatting | bytes 524288

commit v2 on v1

v2 whole, which is shorter than its diff:
```python
import functools

import jax
import jax.numpy as jnp
from jax import lax
from jax.experimental import pallas as pl
from jax.experimental.pallas import tpu as pltpu
from jax.sharding import PartitionSpec as P

MESH = pl.DeviceIdType.MESH
EPS = 1e-05
GROUPS = 1
F32, BF16 = jnp.float32, jnp.bfloat16


def kernel(n, nx, pa_in, ing, lp, lg, rp, rg, og, outg, op, out,
           pa, other, rows_in, gains, gains_other, gain_all, x_all, v_all, wt, wo, gate, y,
           send, left_recv, right_recv, left_all, tri_send, tri_recv, tri_other,
           ready, ready_x, in_sem, ch_send, ch_recv, l_send, l_recv, r_send, r_recv, x_send, x_recv, t_send, t_recv, o_send, o_recv):
    z, x, c = lax.axis_index("row"), lax.axis_index("col"), lax.axis_index("ch")
    ch, rows, lanes = pa.shape
    hp = ch // n
    per_group = hp // GROUPS
    turn = lax.rem(z + n - 1, n)
    bar = pltpu.get_barrier_semaphore()

    def each(lo, hi, f, unroll=None):
        def step(i, carry):
            f(i)
            return carry
        lax.fori_loop(lo, hi, step, 0, unroll=unroll)

    def row_at(i):
        return lax.rem(i + 1, n)

    def turn_of(r):
        return lax.rem(r + n - 1, n)

    def to_core(src, dst, i):
        return pltpu.make_async_remote_copy(src_ref=src, dst_ref=dst, send_sem=ch_send.at[i], recv_sem=ch_recv.at[i],
                                            device_id={"ch": 1 - c}, device_id_type=MESH)

    pl.semaphore_signal(bar, inc=1, device_id={"ch": 1 - c}, device_id_type=MESH)
    loads = [pltpu.make_async_copy(pa_in, pa, in_sem.at[0]),
             pltpu.make_async_copy(ing, rows_in.at[0], in_sem.at[1]),
             pltpu.make_async_copy(outg, rows_in.at[1], in_sem.at[2])]
    for i, w in enumerate((lp, lg, rp, rg, og)):
        loads.append(pltpu.make_async_copy(w, wt.at[pl.ds(i * ch, ch), :], in_sem.at[3 + i]))
    loads.append(pltpu.make_async_copy(op, wo, in_sem.at[8]))
    for load in loads:
        load.start()
    each(0, x, lambda r: pl.semaphore_signal(bar, inc=1, device_id={"col": r}, device_id_type=MESH))
    each(turn + 1, n, lambda i: pl.semaphore_signal(bar, inc=1, device_id={"row": row_at(i)}, device_id_type=MESH))
    pl.semaphore_wait(bar, turn + (nx - 1 - x) + 1)
    raw = to_core(pa_in, other, 0)
    raw.start()
    each(0, turn, lambda i: pl.semaphore_signal(ready.at[z], inc=1, device_id={"row": row_at(i)}, device_id_type=MESH))
    each(x + 1, nx, lambda r: pl.semaphore_signal(ready_x.at[x], inc=1, device_id={"col": r}, device_id_type=MESH))
    for load in loads:
        load.wait()
    for i in range(2):
        gains[i] = jnp.broadcast_to(rows_in[i], (lanes, ch)).T
    gsent = to_core(gains, gains_other, 1)
    gsent.start()
    mine = pl.multiple_of(c * ch, ch)
    theirs = pl.multiple_of((1 - c) * ch, ch)
    raw.wait_recv()
    step_c = 8

    def layer_norm(a, b):
        def add(i, t):
            s = pl.ds(i * step_c, step_c)
            return t + a[s].astype(F32).sum(0) + b[s].astype(F32).sum(0)
        mean = lax.fori_loop(0, ch // step_c, add, jnp.zeros((rows, lanes), F32)) / (2 * ch)

        def sq(i, t):
            s = pl.ds(i * step_c, step_c)
            return t + jnp.square(a[s].astype(F32) - mean).sum(0) + jnp.square(b[s].astype(F32) - mean).sum(0)
        var = lax.fori_loop(0, ch // step_c, sq, jnp.zeros((rows, lanes), F32)) / (2 * ch)
        scale = lax.rsqrt(var + EPS)

        def put(i, carry):
            s = pl.ds(i * step_c, step_c)
            for r, base in ((a, mine), (b, theirs)):
                v = (r[s].astype(F32) - mean) * scale
                x_all[pl.ds(pl.multiple_of((base + i * step_c) * rows, rows * step_c), rows * step_c), :] = v.reshape(rows * step_c, lanes)
            return carry
        lax.fori_loop(0, ch // step_c, put, 0)

    layer_norm(pa, other)
    gsent.wait_recv()
    for i in range(2):
        gain_all[i, pl.ds(mine, ch), :] = gains[i]
        gain_all[i, pl.ds(theirs, ch), :] = gains_other[i]
    def edges(v, i):
        r = jnp.dot(wt[pl.ds(2 * i * ch, 2 * ch), :], v, preferred_element_type=F32)
        return jax.nn.sigmoid(r[ch:]) * r[:ch]

    def lift_left(k):
        v = (x_all[pl.ds(k, 2 * ch, stride=rows), :] * gain_all[0]).astype(BF16)
        v_all[k] = v
        y[pl.ds(k, ch, stride=rows), :] = edges(v, 0)
    each(0, rows, lift_left, 4)

    def pack(side):
        def one(i):
            s = pl.ds(pl.multiple_of(i * hp * rows, hp * rows), hp * rows)
            send[side, i] = y[s, :].reshape(hp, rows, lanes).astype(BF16)
        each(0, n, one, 4)
    pack(0)

    def part(g):
        return pl.ds(g * per_group, per_group)

    def left_copy(r, slot):
        return pltpu.make_async_remote_copy(src_ref=send.at[0, r], dst_ref=left_recv.at[slot], send_sem=l_send, recv_sem=l_recv.at[slot],
                                            device_id={"row": r}, device_id_type=MESH)

    def right_copy(h, r, slot):
        return pltpu.make_async_remote_copy(src_ref=send.at[1, r, part(h)], dst_ref=right_recv.at[h, slot], send_sem=r_send, recv_sem=r_recv.at[h],
                                            device_id={"row": r}, device_id_type=MESH)

    def down(copy):
        def one(i):
            d = n // 2 - i
            r1, r2 = lax.rem(z + d, n), lax.rem(z + n - d, n)

            @pl.when(turn_of(r1) < turn)
            def _():
                copy(r1, z).start()

            @pl.when((turn_of(r2) < turn) & (d < n // 2))
            def _():
                copy(r2, z).start()
        each(0, n // 2, one)
    down(left_copy)
    def lift_right(k):
        y[pl.ds(k, ch, stride=rows), :] = edges(v_all[k], 1)
    each(0, rows, lift_right, 4)
    pack(1)
    for h in range(GROUPS):
        down(functools.partial(right_copy, h))
    left_recv[z] = send[0, z]
    for h in range(GROUPS):
        right_recv[h, z] = send[1, z, h * per_group : (h + 1) * per_group]
    def lift_gate(k):
        gate[k] = jax.nn.sigmoid(jnp.dot(wt[pl.ds(4 * ch, ch), :], v_all[k], preferred_element_type=F32))
    each(0, rows, lift_gate, 4)
    def up_left(i):
        r = row_at(i)
        pl.semaphore_wait(ready.at[r], 1)
        left_copy(r, z).start()

    def up_right(h, i):
        right_copy(h, row_at(i), z).start()

    def up(i):
        up_left(i)
        for h in range(GROUPS):
            up_right(h, i)
    half = jnp.maximum(turn + 1, n // 2)
    each(turn + 1, half, up)
    each(half, n, up_left)
    for h in range(GROUPS):
        each(half, n, functools.partial(up_right, h))

    each(0, x, lambda r: pl.semaphore_wait(ready_x.at[r], 1))

    def to_col(s, r):
        return pltpu.make_async_remote_copy(src_ref=left_recv.at[s], dst_ref=left_all.at[x, s], send_sem=x_send, recv_sem=x_recv.at[x],
                                            device_id={"col": r}, device_id_type=MESH)

    def spread(s):
        @pl.when(s != z)
        def _():
            left_copy(s, s).wait_recv()
        for d in range(1, nx):
            to_col(s, lax.rem(x + d, nx)).start()
        left_all[x, s] = left_recv[s]
    each(0, n, lambda i: spread(row_at(i)))

    def all_rows(src, dst, ss, rs):
        most = pl.ds(0, n - 1)
        return pltpu.make_async_remote_copy(src_ref=src.at[most], dst_ref=dst.at[most], send_sem=ss, recv_sem=rs,
                                            device_id={"row": lax.rem(z + 1, n)}, device_id_type=MESH)

    def whole_col(d):
        r = lax.rem(x + d, nx)
        return pltpu.make_async_remote_copy(src_ref=left_all.at[r], dst_ref=left_all.at[r], send_sem=x_send, recv_sem=x_recv.at[r],
                                            device_id={"col": r}, device_id_type=MESH)
    for d in range(1, nx):
        whole_col(d).wait_recv()
    def tri_copy(h, r, slot):
        return pltpu.make_async_remote_copy(src_ref=tri_send.at[h, r], dst_ref=tri_recv.at[slot, part(h)], send_sem=t_send, recv_sem=t_recv.at[h, slot],
                                            device_id={"row": r}, device_id_type=MESH)

    def swap(h, s):
        return pltpu.make_async_remote_copy(src_ref=tri_recv.at[s, part(h)], dst_ref=tri_other.at[s, part(h)], send_sem=o_send, recv_sem=o_recv,
                                            device_id={"ch": 1 - c}, device_id_type=MESH)

    per = lanes // rows
    for h in range(GROUPS):
        all_rows(right_recv.at[h], right_recv.at[h], r_send, r_recv.at[h]).wait_recv()
        for m in range(per_group):
            right = right_recv[h, :, m].reshape(n * rows, lanes)
            for q in range(nx):
                left = left_all[q, :, h * per_group + m].reshape(n * rows, lanes)
                t = lax.dot_general(left, right, (((0,), (0,)), ((), ())), preferred_element_type=F32)
                tri_send[h, pl.ds(q * per, per), m] = t.reshape(per, rows, lanes).astype(BF16)

        def tri_out(i):
            d = n // 2 - i
            tri_copy(h, lax.rem(z + d, n), z).start()

            @pl.when(d < n // 2)
            def _():
                tri_copy(h, lax.rem(z + n - d, n), z).start()
        each(0, n // 2, tri_out)
        tri_recv[z, h * per_group : (h + 1) * per_group] = tri_send[h, z]

    for h in range(GROUPS):
        swap(h, z).start()

        def tri_in(i):
            d = n // 2 - i
            r1, r2 = lax.rem(z + d, n), lax.rem(z + n - d, n)
            tri_copy(h, r1, r1).wait_recv()
            swap(h, r1).start()

            @pl.when(d < n // 2)
            def _():
                tri_copy(h, r2, r2).wait_recv()
                swap(h, r2).start()
        each(0, n // 2, tri_in)
    swapped = pltpu.make_async_remote_copy(src_ref=tri_recv, dst_ref=tri_other, send_sem=o_send, recv_sem=o_recv,
                                           device_id={"ch": 1 - c}, device_id_type=MESH)
    swapped.wait_recv()
    layer_norm(tri_recv.reshape(ch, rows, lanes), tri_other.reshape(ch, rows, lanes))

    def close(k):
        v = (x_all[pl.ds(k, 2 * ch, stride=rows), :] * gain_all[1]).astype(BF16)
        y[pl.ds(k, ch, stride=rows), :] = jnp.dot(wo[...], v, preferred_element_type=F32) * gate[k]
    each(0, rows, close, 4)
    out[...] = y[...].reshape(ch, rows, lanes).astype(BF16)

    raw.wait_send()
    gsent.wait_send()
    swapped.wait_send()
    all_rows(send.at[0], left_recv, l_send, r_recv.at[0]).wait_send()
    for h in range(GROUPS):
        all_rows(right_recv.at[h], right_recv.at[h], r_send, r_recv.at[h]).wait_send()
        all_rows(tri_send.at[h], tri_send.at[h], t_send, r_recv.at[h]).wait_send()
    for d in range(1, nx):
        whole_col(d).wait_send()


def solution(mesh):
    n, nx = mesh.shape["row"], mesh.shape["col"]

    def per_device(pair_act, in_gain, left_proj, left_gate, right_proj, right_gate, out_gate, out_gain, out_proj):
        ch, rows, lanes = pair_act.shape
        hp = ch // n
        vm = pltpu.VMEM
        dma, reg = pltpu.SemaphoreType.DMA, pltpu.SemaphoreType.REGULAR
        return pl.pallas_call(
            functools.partial(kernel, n, nx),
            out_shape=jax.ShapeDtypeStruct(pair_act.shape, BF16),
            in_specs=[pl.BlockSpec(memory_space=pl.ANY)] * 9,
            out_specs=pl.BlockSpec(memory_space=pltpu.VMEM),
            scratch_shapes=[
                vm((ch, rows, lanes), BF16),
                vm((ch, rows, lanes), BF16),
                vm((2, 1, ch), F32),
                vm((2, ch, lanes), F32),
                vm((2, ch, lanes), F32),
                vm((2, 2 * ch, lanes), F32),
                vm((2 * ch * rows, lanes), F32),
                vm((rows, 2 * ch, lanes), BF16),
                vm((5 * ch, 2 * ch), BF16),
                vm((ch, 2 * ch), BF16),
                vm((rows, ch, lanes), F32),
                vm((ch * rows, lanes), F32),
                vm((2, n, hp, rows, lanes), BF16),
                vm((n, hp, rows, lanes), BF16),
                vm((GROUPS, n, hp // GROUPS, rows, lanes), BF16),
                vm((nx, n, hp, rows, lanes), BF16),
                vm((GROUPS, n, hp // GROUPS, rows, lanes), BF16),
                vm((n, hp, rows, lanes), BF16),
                vm((n, hp, rows, lanes), BF16),
                reg((n,)),
                reg((nx,)),
                dma((9,)),
                dma((2,)),
                dma((2,)),
                dma,
                dma((n,)),
                dma,
                dma((GROUPS,)),
                dma,
                dma((nx,)),
                dma,
                dma((GROUPS, n)),
                dma,
                dma,
            ],
            compiler_params=pltpu.CompilerParams(collective_id=0, has_side_effects=True),
            name="triangle",
        )(pair_act, in_gain[None], left_proj.T, left_gate.T, right_proj.T, right_gate.T, out_gate.T, out_gain[None], out_proj.T)

    return jax.shard_map(
        per_device,
        mesh=mesh,
        in_specs=(
            P("ch", ("grp", "row"), "col"),
            P("ch"),
            P(None, "ch"),
            P(None, "ch"),
            P(None, "ch"),
            P(None, "ch"),
            P(None, "ch"),
            P("ch"),
            P(None, "ch"),
        ),
        out_specs=P("ch", ("grp", "row"), "col"),
        check_vma=False,
    )
```

time: 147 us -> 131 us (0.89)
  the two profiles are of different devices: /device:TPU:35 before, /device:TPU:33 now
where the time goes in v2:
time: 131 us; the launch traced here: 130 us
  Pallas kernels  129 us (98%)
  local copies, waits for them, and re-layouts  1.67 us (1%)
    pallas_call x1, Pallas kernels, per_device(): pl.pallas_call(functools.partial(kernel, n, nx), out_shape=jax.ShapeDtype...  129 us

profile of v2, /device:TPU:33, one launch (start us, length us, event | category | flops | bytes accessed | tf_op | source)
XLA Modules:
  0.0 130.5 jit_solution(8168333784048820918)
XLA Ops:
  0.0 128.8 %triangle.1 = bf16[64,16,128]{2,1,0:T(8,128)(2,1)} custom-call(bf16[64,16,128]{2,1,0:T(8,128)(2,1)} %pa_in.1, f32[1,64]{1,0:T(1,128)} %bitcast.14, bf16[64,128]{1,0:T(8,128)(2,1)} %bitcast.8, bf16[64,128]{1,0:T(8,128)(2,1)} %bitcast.9, bf16[64,128]{1,0:T(8,128)(2,1)} %bitcast.10, bf16[64,128]{1,0:T(8,128)(2,1)} %bitcast.11, bf16[64,128]{1,0:T(8,128)(2,1)} %bitcast.12, ...), custom_call_target="tpu_custom_call" | custom-call | tf_op jit(solution)/shard_map/triangle/pallas_call | solution.py:265
  128.8 1.7 %copy.11 = bf16[64,16,128]{2,1,0:T(8,128)(2,1)} copy(bf16[64,16,128]{2,1,0:T(8,128)(2,1)} %triangle.1) | data formatting | bytes 524288

commit v3 on v2

--- a/solution.py
+++ b/solution.py
@@ -120,50 +120,61 @@
         return pltpu.make_async_remote_copy(src_ref=send.at[1, r, part(h)], dst_ref=right_recv.at[h, slot], send_sem=r_send, recv_sem=r_recv.at[h],
                                             device_id={"row": r}, device_id_type=MESH)
 
-    def down(copy):
-        def one(i):
-            d = n // 2 - i
-            r1, r2 = lax.rem(z + d, n), lax.rem(z + n - d, n)
-
-            @pl.when(turn_of(r1) < turn)
-            def _():
-                copy(r1, z).start()
-
-            @pl.when((turn_of(r2) < turn) & (d < n // 2))
-            def _():
-                copy(r2, z).start()
-        each(0, n // 2, one)
-    down(left_copy)
+    def down_at(copy, i):
+        d = n // 2 - i
+        r1, r2 = lax.rem(z + d, n), lax.rem(z + n - d, n)
+
+        @pl.when(turn_of(r1) < turn)
+        def _():
+            copy(r1, z).start()
+
+        @pl.when((turn_of(r2) < turn) & (d < n // 2))
+        def _():
+            copy(r2, z).start()
+    each(0, n // 2, functools.partial(down_at, left_copy))
     def lift_right(k):
         y[pl.ds(k, ch, stride=rows), :] = edges(v_all[k], 1)
     each(0, rows, lift_right, 4)
     pack(1)
     for h in range(GROUPS):
-        down(functools.partial(right_copy, h))
+        right_recv[h, z] = send[1, z, h * per_group : (h + 1) * per_group]
     left_recv[z] = send[0, z]
-    for h in range(GROUPS):
-        right_recv[h, z] = send[1, z, h * per_group : (h + 1) * per_group]
-    def lift_gate(k):
-        gate[k] = jax.nn.sigmoid(jnp.dot(wt[pl.ds(4 * ch, ch), :], v_all[k], preferred_element_type=F32))
-    each(0, rows, lift_gate, 4)
+
+    def down_right(i):
+        for h in range(GROUPS):
+            down_at(functools.partial(right_copy, h), i)
+
     def up_left(i):
         r = row_at(i)
         pl.semaphore_wait(ready.at[r], 1)
         left_copy(r, z).start()
 
-    def up_right(h, i):
-        right_copy(h, row_at(i), z).start()
+    def up_right(i):
+        for h in range(GROUPS):
+            right_copy(h, row_at(i), z).start()
 
     def up(i):
         up_left(i)
-        for h in range(GROUPS):
-            up_right(h, i)
+        up_right(i)
+    early = turn < n // 2
+    ahead = jnp.where(early, n // 2, 0)
+    each(0, ahead, down_right)
     half = jnp.maximum(turn + 1, n // 2)
     each(turn + 1, half, up)
-    each(half, n, up_left)
-    for h in range(GROUPS):
-        each(half, n, functools.partial(up_right, h))
-
+
+    def mixed(i):
+        up_left(i)
+        t = ahead + i - turn - 1
+
+        @pl.when(t < n // 2)
+        def _():
+            down_right(t)
+    each(half, n, mixed)
+    each(jnp.minimum(ahead + n - half, n // 2), n // 2, down_right)
+    each(half, n, up_right)
+    def lift_gate(k):
+        gate[k] = jax.nn.sigmoid(jnp.dot(wt[pl.ds(4 * ch, ch), :], v_all[k], preferred_element_type=F32))
+    each(0, rows, lift_gate, 4)
     each(0, x, lambda r: pl.semaphore_wait(ready_x.at[r], 1))
 
     def to_col(s, r):
@@ -264,7 +275,7 @@
         dma, reg = pltpu.SemaphoreType.DMA, pltpu.SemaphoreType.REGULAR
         return pl.pallas_call(
             functools.partial(kernel, n, nx),
-            out_shape=jax.ShapeDtypeStruct(pair_act.shape, BF16),
+            out_shape=pltpu.VMEM(pair_act.shape, BF16),
             in_specs=[pl.BlockSpec(memory_space=pl.ANY)] * 9,
             out_specs=pl.BlockSpec(memory_space=pltpu.VMEM),
             scratch_shapes=[

time: 131 us -> 129 us (0.985)
  no operation moved by 1% of the time
where the time goes in v3:
time: 129 us
  Pallas kernels  128 us (99%)
    pallas_call x1, Pallas kernels, per_device(): pl.pallas_call(functools.partial(kernel, n, nx), out_shape=pltpu.VMEM(pai...  128 us

profile of v3, /device:TPU:33, one launch (start us, length us, event | category | flops | bytes accessed | tf_op | source)
XLA Modules:
  0.0 128.8 jit_solution(11384684981874128260)
XLA Ops:
  0.0 128.1 %triangle.1 = bf16[64,16,128]{2,1,0:T(8,128)(2,1)S(1)} custom-call(bf16[64,16,128]{2,1,0:T(8,128)(2,1)} %pa_in.1, f32[1,64]{1,0:T(1,128)} %bitcast.14, bf16[64,128]{1,0:T(8,128)(2,1)} %bitcast.8, bf16[64,128]{1,0:T(8,128)(2,1)} %bitcast.9, bf16[64,128]{1,0:T(8,128)(2,1)} %bitcast.10, bf16[64,128]{1,0:T(8,128)(2,1)} %bitcast.11, bf16[64,128]{1,0:T(8,128)(2,1)} %bitcast.12, ...), custom_call_target="tpu_custom_call" | custom-call | tf_op jit(solution)/shard_map/triangle/pallas_call | solution.py:276
  128.1 0.7 copy.11

commit v4 on v3

--- a/solution.py
+++ b/solution.py
@@ -52,11 +52,12 @@
     each(0, x, lambda r: pl.semaphore_signal(bar, inc=1, device_id={"col": r}, device_id_type=MESH))
     each(turn + 1, n, lambda i: pl.semaphore_signal(bar, inc=1, device_id={"row": row_at(i)}, device_id_type=MESH))
     pl.semaphore_wait(bar, turn + (nx - 1 - x) + 1)
-    raw = to_core(pa_in, other, 0)
+    raw = to_core(pa, other, 0)
+    loads[0].wait()
     raw.start()
     each(0, turn, lambda i: pl.semaphore_signal(ready.at[z], inc=1, device_id={"row": row_at(i)}, device_id_type=MESH))
     each(x + 1, nx, lambda r: pl.semaphore_signal(ready_x.at[x], inc=1, device_id={"col": r}, device_id_type=MESH))
-    for load in loads:
+    for load in loads[1:]:
         load.wait()
     for i in range(2):
         gains[i] = jnp.broadcast_to(rows_in[i], (lanes, ch)).T
@@ -100,7 +101,7 @@
         v = (x_all[pl.ds(k, 2 * ch, stride=rows), :] * gain_all[0]).astype(BF16)
         v_all[k] = v
         y[pl.ds(k, ch, stride=rows), :] = edges(v, 0)
-    each(0, rows, lift_left, 4)
+    each(0, rows, lift_left, 8)
 
     def pack(side):
         def one(i):
@@ -182,13 +183,31 @@
                                             device_id={"col": r}, device_id_type=MESH)
 
     def spread(s):
-        @pl.when(s != z)
-        def _():
-            left_copy(s, s).wait_recv()
         for d in range(1, nx):
             to_col(s, lax.rem(x + d, nx)).start()
         left_all[x, s] = left_recv[s]
-    each(0, n, lambda i: spread(row_at(i)))
+
+    def arrived(s):
+        left_copy(s, s).wait_recv()
+        spread(s)
+    spread(z)
+
+    last = turn >= n - n // 4
+
+    def in_order(i):
+        @pl.when(i != turn)
+        def _():
+            arrived(row_at(i))
+    each(0, jnp.where(last, 0, n), in_order)
+
+    def farthest(i):
+        d = n // 2 - i
+        arrived(lax.rem(z + d, n))
+
+        @pl.when(d < n // 2)
+        def _():
+            arrived(lax.rem(z + n - d, n))
+    each(jnp.where(last, 0, n // 2), n // 2, farthest)
 
     def all_rows(src, dst, ss, rs):
         most = pl.ds(0, n - 1)
@@ -212,21 +231,24 @@
     per = lanes // rows
     for h in range(GROUPS):
         all_rows(right_recv.at[h], right_recv.at[h], r_send, r_recv.at[h]).wait_recv()
-        for m in range(per_group):
-            right = right_recv[h, :, m].reshape(n * rows, lanes)
-            for q in range(nx):
+        rights = [right_recv[h, :, m].reshape(n * rows, lanes) for m in range(per_group)]
+
+        def tri_block(q):
+            for m in range(per_group):
                 left = left_all[q, :, h * per_group + m].reshape(n * rows, lanes)
-                t = lax.dot_general(left, right, (((0,), (0,)), ((), ())), preferred_element_type=F32)
-                tri_send[h, pl.ds(q * per, per), m] = t.reshape(per, rows, lanes).astype(BF16)
-
-        def tri_out(i):
-            d = n // 2 - i
-            tri_copy(h, lax.rem(z + d, n), z).start()
-
-            @pl.when(d < n // 2)
+                t = lax.dot_general(left, rights[m], (((0,), (0,)), ((), ())), preferred_element_type=F32)
+                tri_send[h, pl.ds(pl.multiple_of(q * per, per), per), m] = t.reshape(per, rows, lanes).astype(BF16)
+
+        def tri_to(r):
+            @pl.when(r != z)
             def _():
-                tri_copy(h, lax.rem(z + n - d, n), z).start()
-        each(0, n // 2, tri_out)
+                tri_copy(h, r, z).start()
+
+        def far_block(i):
+            q = lax.rem(z // per + nx // 2 + i, nx)
+            tri_block(q)
+            each(0, per, lambda k: tri_to(q * per + k))
+        each(0, nx, far_block)
         tri_recv[z, h * per_group : (h + 1) * per_group] = tri_send[h, z]
 
     for h in range(GROUPS):

time: 129 us -> 127 us (0.984)
    pallas_call x1, Pallas kernels: 128 us -> 127 us  [per_device(): pl.pallas_call(functools.partial(kernel, n, nx), out_shape=pltpu.VMEM(pai...]
where the time goes in v4:
time: 127 us
  Pallas kernels  127 us (100%)
    pallas_call x1, Pallas kernels, per_device(): pl.pallas_call(functools.partial(kernel, n, nx), out_shape=pltpu.VMEM(pai...  127 us

profile of v4, /device:TPU:33, one launch (start us, length us, event | category | flops | bytes accessed | tf_op | source)
XLA Modules:
  0.0 127.3 jit_solution(7159155632527134308)
XLA Ops:
  0.0 126.6 %triangle.1 = bf16[64,16,128]{2,1,0:T(8,128)(2,1)S(1)} custom-call(bf16[64,16,128]{2,1,0:T(8,128)(2,1)} %pa_in.1, f32[1,64]{1,0:T(1,128)} %bitcast.14, bf16[64,128]{1,0:T(8,128)(2,1)} %bitcast.8, bf16[64,128]{1,0:T(8,128)(2,1)} %bitcast.9, bf16[64,128]{1,0:T(8,128)(2,1)} %bitcast.10, bf16[64,128]{1,0:T(8,128)(2,1)} %bitcast.11, bf16[64,128]{1,0:T(8,128)(2,1)} %bitcast.12, ...), custom_call_target="tpu_custom_call" | custom-call | tf_op jit(solution)/shard_map/triangle/pallas_call | solution.py:298
  126.6 0.7 copy.11

commit v5 on v4

--- a/solution.py
+++ b/solution.py
@@ -244,11 +244,11 @@
             def _():
                 tri_copy(h, r, z).start()
 
-        def far_block(i):
-            q = lax.rem(z // per + nx // 2 + i, nx)
+        def far_block(q):
             tri_block(q)
             each(0, per, lambda k: tri_to(q * per + k))
-        each(0, nx, far_block)
+        for off in sorted(range(nx), key=lambda o: -min(o, nx - o)):
+            far_block(lax.rem(z // per + off, nx))
         tri_recv[z, h * per_group : (h + 1) * per_group] = tri_send[h, z]
 
     for h in range(GROUPS):

time: 127 us -> 126 us (level)
  no operation moved by 1% of the time
where the time goes in v5:
time: 126 us
  Pallas kernels  126 us (100%)
    pallas_call x1, Pallas kernels, per_device(): pl.pallas_call(functools.partial(kernel, n, nx), out_shape=pltpu.VMEM(pai...  126 us

profile of v5, /device:TPU:33, one launch (start us, length us, event | category | flops | bytes accessed | tf_op | source)
XLA Modules:
  0.0 126.2 jit_solution(6555216126040000015)
XLA Ops:
  0.0 125.5 %triangle.1 = bf16[64,16,128]{2,1,0:T(8,128)(2,1)S(1)} custom-call(bf16[64,16,128]{2,1,0:T(8,128)(2,1)} %pa_in.1, f32[1,64]{1,0:T(1,128)} %bitcast.14, bf16[64,128]{1,0:T(8,128)(2,1)} %bitcast.8, bf16[64,128]{1,0:T(8,128)(2,1)} %bitcast.9, bf16[64,128]{1,0:T(8,128)(2,1)} %bitcast.10, bf16[64,128]{1,0:T(8,128)(2,1)} %bitcast.11, bf16[64,128]{1,0:T(8,128)(2,1)} %bitcast.12, ...), custom_call_target="tpu_custom_call" | custom-call | tf_op jit(solution)/shard_map/triangle/pallas_call | solution.py:298
  125.5 0.7 copy.11
